TPU v7x, 32 devices: a whole 2x2x4 slice. The times are simulated.
32 devices in a mesh: gx: 2 (over core), gy: 4 (over y, x), gz: 4 (over z).
Axes of the slice: x: 2, y: 2, z: 4, core: 2. Of those that a mesh axis runs over, the one named last changes fastest.
Arguments:
- block_values: bfloat16 [4, 64, 4, 6, 128, 128], P('gy', 'gx', 'gz'), as said below
- block_cols: int32 [4, 64, 4, 6], P('gy', 'gx', 'gz'), may hold values from 0 to 63, as said below
Outputs:
- purified: float32 [256, 32768], P(('gx', 'gy'), 'gz')
Inputs may be any that keep to these rules, and one draw needn't show every extreme that they name: block_cols[a, s, b, :] holds 6 distinct tile columns of panel b at which tile row a * 64 + s of P is nonzero; every tile column of a panel is listed by exactly 6 tile rows of each slab; the pattern is symmetric: tile (i, j) is listed exactly when tile (j, i) is. `block_values`: P is symmetric: the tile listed at (i, j) is the transpose of the tile listed at (j, i), and diagonal tiles are symmetric.
All inputs are finite; a program needn't handle non-finite values.
Results may differ from a plain program's by a relative error of at most 0.0033.
Values may be sent and summed in bfloat16 or wider, within the bound.
A program may use at most 128 MiB of HBM per device.

v0:
```python
import jax
import jax.numpy as jnp
from jax import lax
from jax.sharding import PartitionSpec as P

WIN = 1


def broadcast(value, axis, source):
    kept = jnp.where(lax.axis_index(axis) == source, value, 0).astype(value.dtype)
    return lax.psum(kept, axis)


def densify(left_tiles, left_columns, slab_tiles):
    onehot = (
        left_columns[:, :, None] == jnp.arange(slab_tiles, dtype=jnp.int32)[None, None, :]
    ).astype(jnp.bfloat16)
    densified = jnp.einsum("wkj,wkyx->wyjx", onehot, left_tiles, preferred_element_type=jnp.float32)
    tile_size = left_tiles.shape[2]
    return densified.astype(jnp.bfloat16).reshape(
        left_tiles.shape[0] * tile_size, slab_tiles, tile_size
    )


def product_one(left_panel, panel_tiles, panel_columns):
    summed = jnp.zeros(
        (left_panel.shape[0], panel_tiles.shape[0], panel_tiles.shape[2]), jnp.float32
    )
    for column_slot in range(panel_tiles.shape[1]):
        picked = jnp.take(left_panel, panel_columns[:, column_slot], axis=1)
        summed = summed + jnp.einsum(
            "rix,iyx->riy", picked, panel_tiles[:, column_slot], preferred_element_type=jnp.float32
        )
    return summed


def product_two(rounded, panel_tiles, panel_columns, panel_width):
    summed = jnp.zeros((rounded.shape[0], panel_width, panel_tiles.shape[3]), jnp.float32)
    for column_slot in range(panel_tiles.shape[1]):
        product = jnp.einsum(
            "rix,ixy->riy", rounded, panel_tiles[:, column_slot], preferred_element_type=jnp.float32
        )
        summed = summed.at[:, panel_columns[:, column_slot], :].add(product)
    return summed


def local(block_values, block_cols):
    tiles_here = block_values[0, :, 0]
    columns_here = block_cols[0, :, 0]
    tile_size = tiles_here.shape[2]
    slab_tiles = tiles_here.shape[0] * lax.axis_size("gx")
    left_tiles, left_columns = (
        broadcast(tiles_here[:WIN], "gy", 0),
        broadcast(columns_here[:WIN], "gy", 0),
    )
    left_panel = densify(left_tiles, left_columns, slab_tiles)
    height = left_panel.shape[0]
    on_diagonal = (lax.axis_index("gy") == lax.axis_index("gz")).astype(jnp.float32)
    panel_tiles, panel_columns = (
        lax.all_gather(tiles_here, "gx", axis=0, tiled=True),
        lax.all_gather(columns_here, "gx", axis=0, tiled=True),
    )
    partial_square = product_one(left_panel, panel_tiles, panel_columns)
    partial_square = partial_square.reshape(height, slab_tiles * tile_size)
    square = lax.psum(partial_square, "gz")
    square_low = square.astype(jnp.bfloat16).reshape(height, slab_tiles, tile_size)
    applied = product_two(square_low, panel_tiles, panel_columns, slab_tiles).reshape(
        lax.axis_size("gy") * (height // lax.axis_size("gy")), slab_tiles * tile_size
    )
    return lax.psum_scatter(
        3.0 * on_diagonal * square - 2.0 * applied, "gy", scatter_dimension=0, tiled=True
    )


def solution(mesh):
    in_specs = (P("gy", "gx", "gz", None, None, None), P("gy", "gx", "gz", None))
    out_specs = P(("gx", "gy"), "gz")
    return jax.shard_map(local, mesh=mesh, in_specs=in_specs, out_specs=out_specs, check_vma=False)
```

profile of v0, /device:TPU:0, one launch (start us, length us, event | category | flops | bytes accessed | tf_op | source)
XLA Modules:
  0.0 449.8 jit_solution(1277576746980991775)
XLA Ops:
  7.4 0.9 slice.56
  8.3 0.8 fusion.35
  9.2 0.0 all-gather.4.cloned.1.call-start
  9.2 8.0 %copy.48 = bf16[1,32,1,6,128,128]{5,4,1,3,2,0:T(8,128)(2,1)} copy(bf16[1,32,1,6,128,128]{5,4,3,2,1,0:T(8,128)(2,1)} %param.4) | data formatting | bytes 12582912 | tf_op args[0]
  17.3 0.0 all-gather.4.cloned.1.call-update
  17.3 0.0 all-reduce.5.cloned.1.call-start
  17.4 0.6 copy-done.5
  18.0 0.2 fusion.44
  18.2 8.9 %psum.25 = s32[6]{0:T(128)S(1)} all-reduce(s32[6]{0:T(128)S(1)} %fusion.44), channel_id=1, replica_groups=mesh['gx'=2,'gy'=4,'gz'=4] {'gy'}, use_global_device_ids=true, to_apply=%region_1.2 | all-reduce | flops 6 | bytes 48 | tf_op jit(solution)/shard_map/psum | solution.py:11
  27.1 0.1 copy.45
  27.1 1.8 all-gather
  29.0 0.4 fusion.41
  29.5 27.4 %all-reduce.3.cloned.1.call-done = bf16[6,128,128]{2,0,1:T(8,128)(2,1)} async-done(((bf16[6,128,128]{2,0,1:T(8,128)(2,1)}), bf16[6,128,128]{2,0,1:T(8,128)(2,1)}) %all-reduce.3.cloned.1.call-update) | async-done | bytes 196624 | tf_op jit(solution)/shard_map/psum | solution.py:11
  56.9 1.8 convert_bitcast_fusion
  58.7 1.4 copy.47
  60.0 2.2 gather_fusion.4
  62.2 2.1 gather_fusion.3
  64.4 2.2 gather_fusion.2
  66.5 2.1 gather_fusion.1
  68.7 2.2 gather_fusion
  70.8 2.1 gather_fusion.5
  73.0 6.2 %fusion.1 = f32[64,128,128]{1,2,0:T(8,128)} fusion(bf16[64,128,128]{2,1,0:T(8,128)(2,1)} %gather_fusion.4, pred[64]{0:T(512)(128)(4,1)S(1)} %get-tuple-element.24, bf16[64,6,128,128]{3,2,0,1:T(8,128)(2,1)} %bitcast.77), kind=kOutput, calls=%fused_computation.21 | convolution fusion | flops 269484032 | bytes 8388672 | tf_op jit(solution)/shard_map/rix,iyx->riy/dot_general | solution.py:31
  79.1 6.0 %fusion.3 = f32[64,128,128]{1,2,0:T(8,128)} fusion(bf16[64,128,128]{2,1,0:T(8,128)(2,1)} %gather_fusion.3, pred[64]{0:T(512)(128)(4,1)S(1)} %get-tuple-element.25, bf16[64,6,128,128]{3,2,0,1:T(8,128)(2,1)} %bitcast.78), kind=kOutput, calls=%fused_computation.23 | convolution fusion | flops 269484032 | bytes 8388672 | tf_op jit(solution)/shard_map/rix,iyx->riy/dot_general | solution.py:31
  85.2 3.6 fusion.5
  88.8 3.6 fusion.7
  92.4 3.6 fusion.9
  96.0 10.1 %add_add_fusion = f32[64,128,128]{1,2,0:T(8,128)} fusion(f32[64,128,128]{1,2,0:T(8,128)} %fusion.1, f32[64,128,128]{1,2,0:T(8,128)} %fusion.3, f32[64,128,128]{1,2,0:T(8,128)} %fusion.5, f32[64,128,128]{1,2,0:T(8,128)} %fusion.9, f32[64,128,128]{1,2,0:T(8,128)} %fusion.7, bf16[64,128,128]{2,1,0:T(8,128)(2,1)S(1)} %copy-done.4, ...), kind=kOutput, calls=%fused_computation.13 | convolution fusion | flops 274726912 | bytes 29360640 | tf_op jit(solution)/shard_map/rix,iyx->riy/dot_general | solution.py:31
  106.1 0.2 reduce-scatter.4.cloned.1.call-start
  106.4 154.9 %all-reduce.5.cloned.1.call-done = f32[128,8192]{0,1:T(8,128)} async-done(((f32[128,8192]{0,1:T(8,128)}), f32[128,8192]{0,1:T(8,128)}) %all-reduce.5.cloned.1.call-update) | async-done | bytes 4194320 | tf_op jit(solution)/shard_map/psum | solution.py:65
  261.3 2.5 convert_element_type.19
  263.8 4.5 %fusion.24 = f32[64,128,128]{2,1,0:T(8,128)} fusion(bf16[128,64,128]{0,2,1:T(8,128)(2,1)S(1)} %bitcast.71, bf16[64,6,128,128]{3,2,0,1:T(8,128)(2,1)} %bitcast.79), kind=kOutput, calls=%fused_computation.46 | convolution fusion | flops 268435456 | bytes 8388608 | tf_op jit(solution)/shard_map/rix,ixy->riy/dot_general | solution.py:40
  268.4 4.6 %fusion.23 = f32[64,128,128]{2,1,0:T(8,128)} fusion(bf16[128,64,128]{0,2,1:T(8,128)(2,1)S(1)} %bitcast.72, bf16[64,6,128,128]{3,2,0,1:T(8,128)(2,1)} %bitcast.80), kind=kOutput, calls=%fused_computation.45 | convolution fusion | flops 268435456 | bytes 8388608 | tf_op jit(solution)/shard_map/rix,ixy->riy/dot_general | solution.py:40
  272.9 2.8 fusion.25
  275.8 2.8 fusion.26
  278.6 2.8 fusion.27
  281.4 2.8 fusion.28
  284.2 2.5 broadcast_in_dim.30
  286.7 13.9 %scatter_fusion = f32[128,64,128]{2,0,1:T(8,128)} fusion(f32[128,64,128]{2,0,1:T(8,128)} %broadcast_in_dim.30, s32[64]{0:T(128)S(1)} %get-tuple-element.7, f32[64,128,128]{2,1,0:T(8,128)} %fusion.23), kind=kCustom, calls=%fused_computation.6 | custom fusion | flops 1048576 | bytes 12583168 | tf_op jit(solution)/shard_map/scatter-add | solution.py:43
  300.6 13.6 %scatter_fusion.1 = f32[128,64,128]{2,0,1:T(8,128)} fusion(f32[128,64,128]{2,0,1:T(8,128)} %scatter_fusion, s32[64]{0:T(128)S(1)} %get-tuple-element.8, f32[64,128,128]{2,1,0:T(8,128)} %fusion.24), kind=kCustom, calls=%fused_computation.7 | custom fusion | flops 1048576 | bytes 12583168 | tf_op jit(solution)/shard_map/scatter-add | solution.py:43
  314.2 13.6 %scatter_fusion.2 = f32[128,64,128]{2,0,1:T(8,128)} fusion(f32[128,64,128]{2,0,1:T(8,128)} %scatter_fusion.1, s32[64]{0:T(128)S(1)} %get-tuple-element.9, f32[64,128,128]{2,1,0:T(8,128)} %fusion.25), kind=kCustom, calls=%fused_computation.8 | custom fusion | flops 1048576 | bytes 12583168 | tf_op jit(solution)/shard_map/scatter-add | solution.py:43
  327.9 13.7 %scatter_fusion.3 = f32[128,64,128]{2,0,1:T(8,128)} fusion(f32[128,64,128]{2,0,1:T(8,128)} %scatter_fusion.2, s32[64]{0:T(128)S(1)} %get-tuple-element.10, f32[64,128,128]{2,1,0:T(8,128)} %fusion.26), kind=kCustom, calls=%fused_computation.9 | custom fusion | flops 1048576 | bytes 12583168 | tf_op jit(solution)/shard_map/scatter-add | solution.py:43
  341.6 13.7 %scatter_fusion.4 = f32[128,64,128]{2,0,1:T(8,128)} fusion(f32[128,64,128]{2,0,1:T(8,128)} %scatter_fusion.3, s32[64]{0:T(128)S(1)} %get-tuple-element.11, f32[64,128,128]{2,1,0:T(8,128)} %fusion.27), kind=kCustom, calls=%fused_computation.10 | custom fusion | flops 1048576 | bytes 12583168 | tf_op jit(solution)/shard_map/scatter-add | solution.py:43
  355.2 13.6 %scatter_fusion.5 = f32[128,64,128]{2,0,1:T(8,128)} fusion(f32[128,64,128]{2,0,1:T(8,128)} %scatter_fusion.4, s32[64]{0:T(128)S(1)} %get-tuple-element.6, f32[64,128,128]{2,1,0:T(8,128)} %fusion.28), kind=kCustom, calls=%fused_computation.11 | custom fusion | flops 1048576 | bytes 12583168 | tf_op jit(solution)/shard_map/scatter-add | solution.py:43
  368.9 4.7 %broadcast_multiply_fusion = f32[128,64,128]{2,0,1:T(8,128)} fusion(f32[128,64,128]{2,0,1:T(8,128)} %scatter_fusion.5), kind=kLoop, calls=%fused_computation.37 | loop fusion | flops 1048576 | bytes 8388608 | tf_op jit(solution)/shard_map/mul | solution.py:71
  373.6 5.6 %copy.60 = f32[128,64,128]{0,2,1:T(8,128)} copy(f32[128,64,128]{2,0,1:T(8,128)} %broadcast_multiply_fusion) | data formatting | bytes 8388608 | tf_op jit(solution)/shard_map/mul | solution.py:71
  379.2 5.8 %bitcast_subtract_fusion = f32[128,8192]{0,1:T(8,128)} fusion(f32[128,64,128]{0,2,1:T(8,128)} %copy.60, f32[128,8192]{0,1:T(8,128)} %all-reduce.5.cloned.1.call-done, f32[]{:T(128)S(6)} %mul_shard_map.3), kind=kLoop, calls=%fused_computation.12 | loop fusion | flops 2097152 | bytes 12582916 | tf_op jit(solution)/shard_map/sub | solution.py:71
  385.1 5.6 %copy.68 = f32[128,8192]{1,0:T(8,128)} copy(f32[128,8192]{0,1:T(8,128)} %bitcast_subtract_fusion) | data formatting | bytes 8388608
  390.7 51.9 %reduce-scatter.4.cloned.1.call-done = f32[32,8192]{1,0:T(8,128)} async-done(((f32[128,8192]{1,0:T(8,128)}), f32[32,8192]{1,0:T(8,128)}) %reduce-scatter.4.cloned.1.call-update) | async-done | bytes 1048592 | tf_op jit(solution)/shard_map/reduce_scatter | solution.py:70
  (36 shorter events, 0.2 us)
Async XLA Ops:
  7.4 49.5 %all-reduce.3.cloned.1.call-start = ((), (), s32[]{:S(2)}) async-start(), calls=%async_computation.1 | async-start | bytes 524288 | tf_op jit(solution)/shard_map/psum | solution.py:11
  9.2 63.8 %all-gather.4.cloned.1.call-start = ((), (), s32[]{:S(2)}) async-start(), calls=%async_computation.3 | async-start | bytes 18874368 | tf_op jit(solution)/shard_map/all_gather | solution.py:60
  17.3 0.7 copy-start.5
  17.3 244.0 %all-reduce.5.cloned.1.call-start = ((), (), s32[]{:S(2)}) async-start(), calls=%async_computation.2 | async-start | bytes 8388608 | tf_op jit(solution)/shard_map/psum | solution.py:65
  73.0 12.2 %copy-start = (bf16[1,64,1,6,128,128]{5,4,1,3,2,0:T(8,128)(2,1)S(1)}, bf16[1,64,1,6,128,128]{5,4,1,3,2,0:T(8,128)(2,1)}, u32[]{:S(2)}) copy-start(bf16[1,64,1,6,128,128]{5,4,1,3,2,0:T(8,128)(2,1)} %all-gather.4.cloned.1.call-done) | copy-start | bytes 37748740
  79.1 6.0 %copy-start.3 = (bf16[64,128,128]{2,1,0:T(8,128)(2,1)S(1)}, bf16[64,128,128]{2,1,0:T(8,128)(2,1)}, u32[]{:S(2)}) copy-start(bf16[64,128,128]{2,1,0:T(8,128)(2,1)} %gather_fusion.2) | copy-start | bytes 6291460
  85.2 3.6 copy-start.2
  88.8 3.6 copy-start.1
  92.4 3.6 copy-start.4
  106.1 336.5 %reduce-scatter.4.cloned.1.call-start = ((), (), s32[]{:S(2)}) async-start(), calls=%async_computation.4 | async-start | bytes 5242880 | tf_op jit(solution)/shard_map/reduce_scatter | solution.py:70
  261.3 11.7 %slice-start = ((s8[12582912]{0:T(1024)(128)(4,1)}), s8[4194304]{0:T(1024)(128)(4,1)S(1)}, s32[]{:S(2)}) async-start(s8[12582912]{0:T(1024)(128)(4,1)} %bitcast.85), calls=%async_computation.5 | async-start | bytes 8388608
  263.8 9.1 %slice-start.1 = ((s8[12582912]{0:T(1024)(128)(4,1)}), s8[4194304]{0:T(1024)(128)(4,1)S(1)}, s32[]{:S(2)}) async-start(s8[12582912]{0:T(1024)(128)(4,1)} %bitcast.85), calls=%async_computation.6 | async-start | bytes 8388608
  268.3 4.6 %slice-start.2 = ((s8[12582912]{0:T(1024)(128)(4,1)}), s8[4194304]{0:T(1024)(128)(4,1)S(1)}, s32[]{:S(2)}) async-start(s8[12582912]{0:T(1024)(128)(4,1)} %bitcast.85), calls=%async_computation.7 | async-start | bytes 8388608
Sparse Core Ops, SparseCore 0:
  11.1 45.7 all-reduce.2
  106.3 154.9 all-reduce.4
  390.8 51.7 reduce-scatter.3
Sparse Core Ops, SparseCore 1:
  17.4 27.3 all-gather.3
where the time goes:
time: 451 us; the launch traced here: 450 us
  waiting for transfers between devices  234 us (52%)
  other arithmetic  96.8 us (21%)
  matrix products  55.3 us (12%)
  local copies, waits for them, and re-layouts  37.7 us (8%)
  between operations  14.7 us (3%)
  blocking collectives  10.7 us (2%)
    psum x1, waiting for transfers between devices, local(): square = lax.psum(partial_square, 'gz')  155 us
    scatter-add x6, other arithmetic, product_two(): summed = summed.at[:, panel_columns[:, column_slot], :].add(product)  82.2 us
    reduce_scatter x1, waiting for transfers between devices, local(): lax.psum_scatter(3.0 * on_diagonal * square - 2.0 * applied, 'gy', scatte...  51.9 us
    dot_general x6, matrix products, product_one(): jnp.einsum('rix,iyx->riy', picked, panel_tiles[:, column_slot], preferred...  33.1 us
    psum x1, waiting for transfers between devices, broadcast(): return lax.psum(kept, axis)  27.4 us
    dot_general x6, matrix products, product_two(): jnp.einsum('rix,ixy->riy', rounded, panel_tiles[:, column_slot], preferre...  20.4 us
    unnamed x21, local copies, waits for them, and re-layouts  14.4 us
    gather x6, local copies, waits for them, and re-layouts, product_one(): picked = jnp.take(left_panel, panel_columns[:, column_slot], axis=1)  12.9 us
  transfers between devices with their start and end apart: 4, of which 3 were waited for; matrix products, arithmetic and copies ran while one was open for 6% of the time, Pallas kernels for 0%

commit v1 on v0

--- a/solution.py
+++ b/solution.py
@@ -8,7 +8,7 @@
 
 def broadcast(value, axis, source):
     kept = jnp.where(lax.axis_index(axis) == source, value, 0).astype(value.dtype)
-    return lax.psum(kept, axis)
+    return jnp.sum(jax.lax.all_gather(kept, axis), axis=0)
 
 
 def densify(left_tiles, left_columns, slab_tiles):

time: 451 us -> 434 us (0.962)
  waiting for transfers between devices: 234 us -> 207 us
  blocking collectives: 10.7 us -> 23.5 us
    psum x1 -> x0, waiting for transfers between devices: 27.4 us -> none  [broadcast(): return lax.psum(kept, axis)]
    all_gather x0 -> x2, blocking collectives: none -> 21.5 us  [broadcast(): return jnp.sum(jax.lax.all_gather(kept, axis), axis=0)]
    psum x1 -> x0, blocking collectives: 8.89 us -> none  [broadcast(): return lax.psum(kept, axis)]
    unnamed x21 -> x22, local copies, waits for them, and re-layouts: 14.4 us -> 14.5 us
  transfers between devices with their start and end apart: 4 -> 3, of which waited for: 3 -> 2; matrix products, arithmetic and copies ran while one was open for 6% -> 4% of each run, Pallas kernels for 0% -> 0%
where the time goes in v1:
time: 434 us; the launch traced here: 432 us
  waiting for transfers between devices  207 us (48%)
  other arithmetic  97 us (22%)
  matrix products  54.3 us (13%)
  local copies, waits for them, and re-layouts  36.8 us (8%)
  blocking collectives  23.5 us (5%)
  between operations  13.2 us (3%)
    psum x1, waiting for transfers between devices, local(): square = lax.psum(partial_square, 'gz')  155 us
    scatter-add x6, other arithmetic, product_two(): summed = summed.at[:, panel_columns[:, column_slot], :].add(product)  82.2 us
    reduce_scatter x1, waiting for transfers between devices, local(): lax.psum_scatter(3.0 * on_diagonal * square - 2.0 * applied, 'gy', scatte...  51.9 us
    dot_general x6, matrix products, product_one(): jnp.einsum('rix,iyx->riy', picked, panel_tiles[:, column_slot], preferred...  33.1 us
    all_gather x2, blocking collectives, broadcast(): return jnp.sum(jax.lax.all_gather(kept, axis), axis=0)  21.5 us
    dot_general x6, matrix products, product_two(): jnp.einsum('rix,ixy->riy', rounded, panel_tiles[:, column_slot], preferre...  20.4 us
    unnamed x22, local copies, waits for them, and re-layouts  14.5 us
    gather x6, local copies, waits for them, and re-layouts, product_one(): picked = jnp.take(left_panel, panel_columns[:, column_slot], axis=1)  12.9 us
  transfers between devices with their start and end apart: 3, of which 2 were waited for; matrix products, arithmetic and copies ran while one was open for 4% of the time, Pallas kernels for 0%

profile of v1, /device:TPU:0, one launch (start us, length us, event | category | flops | bytes accessed | tf_op | source)
XLA Modules:
  0.0 432.4 jit_solution(15019416371879716149)
XLA Ops:
  6.5 8.0 %copy.48 = bf16[1,32,1,6,128,128]{5,4,1,3,2,0:T(8,128)(2,1)} copy(bf16[1,32,1,6,128,128]{5,4,3,2,1,0:T(8,128)(2,1)} %param.4) | data formatting | bytes 12582912 | tf_op args[0]
  14.6 0.0 all-gather.6.cloned.1.call-update
  14.6 0.0 all-reduce.2.cloned.1.call-start
  14.7 0.6 copy-done.5
  15.3 0.1 copy.70
  15.4 9.4 %all-gather.1 = s32[4,1,1,6]{3,2,1,0:T(1,128)S(1)} all-gather(s32[1,1,1,6]{3,2,1,0:T(1,128)S(1)} %broadcast_select_fusion), channel_id=3, replica_groups=mesh['gx'=2,'gy'=4,'gz'=4] {'gy'}, dimensions={0}, use_global_device_ids=true | all-gather | bytes 120 | tf_op jit(solution)/shard_map/all_gather | solution.py:11
  24.8 0.1 copy.44
  24.9 1.0 slice_select_fusion
  25.9 12.1 %all-gather = bf16[4,1,1,6,128,128]{5,4,3,2,1,0:T(8,128)(2,1)S(1)} all-gather(bf16[1,1,1,6,128,128]{5,4,3,2,1,0:T(8,128)(2,1)S(1)} %slice_select_fusion), channel_id=2, replica_groups=mesh['gx'=2,'gy'=4,'gz'=4] {'gy'}, dimensions={0}, use_global_device_ids=true | all-gather | bytes 983040 | tf_op jit(solution)/shard_map/all_gather | solution.py:11
  38.0 0.1 reduce.3
  38.1 0.8 convert_bitcast_fusion
  39.0 1.4 copy.47
  40.3 2.0 all-gather.2
  42.4 0.4 fusion.41
  42.8 2.2 gather_fusion.4
  45.0 2.1 gather_fusion.3
  47.1 2.2 gather_fusion.2
  49.3 2.1 gather_fusion.1
  51.4 2.2 gather_fusion
  53.6 2.1 gather_fusion.5
  55.8 0.0 all-gather.6.cloned.1.call-done
  55.8 6.2 %fusion.1 = f32[64,128,128]{1,2,0:T(8,128)} fusion(bf16[64,128,128]{2,1,0:T(8,128)(2,1)} %gather_fusion.4, pred[64]{0:T(512)(128)(4,1)S(1)} %get-tuple-element.25, bf16[64,6,128,128]{3,2,0,1:T(8,128)(2,1)} %bitcast.73), kind=kOutput, calls=%fused_computation.21 | convolution fusion | flops 269484032 | bytes 8388672 | tf_op jit(solution)/shard_map/rix,iyx->riy/dot_general | solution.py:31
  62.0 6.0 %fusion.3 = f32[64,128,128]{1,2,0:T(8,128)} fusion(bf16[64,128,128]{2,1,0:T(8,128)(2,1)} %gather_fusion.3, pred[64]{0:T(512)(128)(4,1)S(1)} %get-tuple-element.26, bf16[64,6,128,128]{3,2,0,1:T(8,128)(2,1)} %bitcast.74), kind=kOutput, calls=%fused_computation.23 | convolution fusion | flops 269484032 | bytes 8388672 | tf_op jit(solution)/shard_map/rix,iyx->riy/dot_general | solution.py:31
  68.0 3.6 fusion.5
  71.7 3.6 fusion.7
  75.3 3.6 fusion.9
  78.9 10.1 %add_add_fusion = f32[64,128,128]{1,2,0:T(8,128)} fusion(f32[64,128,128]{1,2,0:T(8,128)} %fusion.1, f32[64,128,128]{1,2,0:T(8,128)} %fusion.3, f32[64,128,128]{1,2,0:T(8,128)} %fusion.5, f32[64,128,128]{1,2,0:T(8,128)} %fusion.9, f32[64,128,128]{1,2,0:T(8,128)} %fusion.7, bf16[64,128,128]{2,1,0:T(8,128)(2,1)S(1)} %copy-done.4, ...), kind=kOutput, calls=%fused_computation.13 | convolution fusion | flops 274726912 | bytes 29360640 | tf_op jit(solution)/shard_map/rix,iyx->riy/dot_general | solution.py:31
  89.0 0.3 reduce-scatter.4.cloned.1.call-start
  89.3 155.2 %all-reduce.2.cloned.1.call-done = f32[128,8192]{0,1:T(8,128)} async-done(((f32[128,8192]{0,1:T(8,128)}), f32[128,8192]{0,1:T(8,128)}) %all-reduce.2.cloned.1.call-update) | async-done | bytes 4194320 | tf_op jit(solution)/shard_map/psum | solution.py:65
  244.4 2.5 convert_element_type.21
  247.0 4.5 %fusion.24 = f32[64,128,128]{2,1,0:T(8,128)} fusion(bf16[128,64,128]{0,2,1:T(8,128)(2,1)S(1)} %bitcast.67, bf16[64,6,128,128]{3,2,0,1:T(8,128)(2,1)} %bitcast.75), kind=kOutput, calls=%fused_computation.46 | convolution fusion | flops 268435456 | bytes 8388608 | tf_op jit(solution)/shard_map/rix,ixy->riy/dot_general | solution.py:40
  251.5 4.6 %fusion.23 = f32[64,128,128]{2,1,0:T(8,128)} fusion(bf16[128,64,128]{0,2,1:T(8,128)(2,1)S(1)} %bitcast.68, bf16[64,6,128,128]{3,2,0,1:T(8,128)(2,1)} %bitcast.76), kind=kOutput, calls=%fused_computation.45 | convolution fusion | flops 268435456 | bytes 8388608 | tf_op jit(solution)/shard_map/rix,ixy->riy/dot_general | solution.py:40
  256.1 2.8 fusion.25
  259.0 2.8 fusion.26
  261.8 2.8 fusion.27
  264.6 2.8 fusion.28
  267.4 2.5 broadcast_in_dim.30
  269.9 14.0 %scatter_fusion = f32[128,64,128]{2,0,1:T(8,128)} fusion(f32[128,64,128]{2,0,1:T(8,128)} %broadcast_in_dim.30, s32[64]{0:T(128)S(1)} %get-tuple-element.7, f32[64,128,128]{2,1,0:T(8,128)} %fusion.23), kind=kCustom, calls=%fused_computation.6 | custom fusion | flops 1048576 | bytes 12583168 | tf_op jit(solution)/shard_map/scatter-add | solution.py:43
  283.8 13.6 %scatter_fusion.1 = f32[128,64,128]{2,0,1:T(8,128)} fusion(f32[128,64,128]{2,0,1:T(8,128)} %scatter_fusion, s32[64]{0:T(128)S(1)} %get-tuple-element.8, f32[64,128,128]{2,1,0:T(8,128)} %fusion.24), kind=kCustom, calls=%fused_computation.7 | custom fusion | flops 1048576 | bytes 12583168 | tf_op jit(solution)/shard_map/scatter-add | solution.py:43
  297.5 13.6 %scatter_fusion.2 = f32[128,64,128]{2,0,1:T(8,128)} fusion(f32[128,64,128]{2,0,1:T(8,128)} %scatter_fusion.1, s32[64]{0:T(128)S(1)} %get-tuple-element.9, f32[64,128,128]{2,1,0:T(8,128)} %fusion.25), kind=kCustom, calls=%fused_computation.8 | custom fusion | flops 1048576 | bytes 12583168 | tf_op jit(solution)/shard_map/scatter-add | solution.py:43
  311.1 13.7 %scatter_fusion.3 = f32[128,64,128]{2,0,1:T(8,128)} fusion(f32[128,64,128]{2,0,1:T(8,128)} %scatter_fusion.2, s32[64]{0:T(128)S(1)} %get-tuple-element.10, f32[64,128,128]{2,1,0:T(8,128)} %fusion.26), kind=kCustom, calls=%fused_computation.9 | custom fusion | flops 1048576 | bytes 12583168 | tf_op jit(solution)/shard_map/scatter-add | solution.py:43
  324.8 13.7 %scatter_fusion.4 = f32[128,64,128]{2,0,1:T(8,128)} fusion(f32[128,64,128]{2,0,1:T(8,128)} %scatter_fusion.3, s32[64]{0:T(128)S(1)} %get-tuple-element.11, f32[64,128,128]{2,1,0:T(8,128)} %fusion.27), kind=kCustom, calls=%fused_computation.10 | custom fusion | flops 1048576 | bytes 12583168 | tf_op jit(solution)/shard_map/scatter-add | solution.py:43
  338.4 13.6 %scatter_fusion.5 = f32[128,64,128]{2,0,1:T(8,128)} fusion(f32[128,64,128]{2,0,1:T(8,128)} %scatter_fusion.4, s32[64]{0:T(128)S(1)} %get-tuple-element.6, f32[64,128,128]{2,1,0:T(8,128)} %fusion.28), kind=kCustom, calls=%fused_computation.11 | custom fusion | flops 1048576 | bytes 12583168 | tf_op jit(solution)/shard_map/scatter-add | solution.py:43
  352.1 4.7 %broadcast_multiply_fusion = f32[128,64,128]{2,0,1:T(8,128)} fusion(f32[128,64,128]{2,0,1:T(8,128)} %scatter_fusion.5), kind=kLoop, calls=%fused_computation.37 | loop fusion | flops 1048576 | bytes 8388608 | tf_op jit(solution)/shard_map/mul | solution.py:71
  356.8 5.6 %copy.60 = f32[128,64,128]{0,2,1:T(8,128)} copy(f32[128,64,128]{2,0,1:T(8,128)} %broadcast_multiply_fusion) | data formatting | bytes 8388608 | tf_op jit(solution)/shard_map/mul | solution.py:71
  362.4 5.8 %bitcast_subtract_fusion = f32[128,8192]{0,1:T(8,128)} fusion(f32[128,64,128]{0,2,1:T(8,128)} %copy.60, f32[128,8192]{0,1:T(8,128)} %all-reduce.2.cloned.1.call-done, f32[]{:T(128)S(6)} %mul_shard_map.3), kind=kLoop, calls=%fused_computation.12 | loop fusion | flops 2097152 | bytes 12582916 | tf_op jit(solution)/shard_map/sub | solution.py:71
  368.3 5.6 %copy.68 = f32[128,8192]{1,0:T(8,128)} copy(f32[128,8192]{0,1:T(8,128)} %bitcast_subtract_fusion) | data formatting | bytes 8388608
  373.9 51.9 %reduce-scatter.4.cloned.1.call-done = f32[32,8192]{1,0:T(8,128)} async-done(((f32[128,8192]{1,0:T(8,128)}), f32[32,8192]{1,0:T(8,128)}) %reduce-scatter.4.cloned.1.call-update) | async-done | bytes 1048592 | tf_op jit(solution)/shard_map/reduce_scatter | solution.py:70
  (35 shorter events, 0.2 us)
Async XLA Ops:
  6.5 49.3 %all-gather.6.cloned.1.call-start = ((), (), s32[]{:S(2)}) async-start(), calls=%async_computation.2 | async-start | bytes 18874368 | tf_op jit(solution)/shard_map/all_gather | solution.py:60
  14.6 0.7 copy-start.5
  14.6 229.8 %all-reduce.2.cloned.1.call-start = ((), (), s32[]{:S(2)}) async-start(), calls=%async_computation.1 | async-start | bytes 8388608 | tf_op jit(solution)/shard_map/psum | solution.py:65
  55.8 12.2 %copy-start = (bf16[1,64,1,6,128,128]{5,4,1,3,2,0:T(8,128)(2,1)S(1)}, bf16[1,64,1,6,128,128]{5,4,1,3,2,0:T(8,128)(2,1)}, u32[]{:S(2)}) copy-start(bf16[1,64,1,6,128,128]{5,4,1,3,2,0:T(8,128)(2,1)} %all-gather.6.cloned.1.call-done) | copy-start | bytes 37748740
  62.0 6.0 %copy-start.1 = (bf16[64,128,128]{2,1,0:T(8,128)(2,1)S(1)}, bf16[64,128,128]{2,1,0:T(8,128)(2,1)}, u32[]{:S(2)}) copy-start(bf16[64,128,128]{2,1,0:T(8,128)(2,1)} %gather_fusion.2) | copy-start | bytes 6291460
  68.0 3.6 copy-start.2
  71.6 3.6 copy-start.3
  75.3 3.6 copy-start.4
  89.0 336.9 %reduce-scatter.4.cloned.1.call-start = ((), (), s32[]{:S(2)}) async-start(), calls=%async_computation.3 | async-start | bytes 5242880 | tf_op jit(solution)/shard_map/reduce_scatter | solution.py:70
  244.4 11.7 %slice-start = ((s8[12582912]{0:T(1024)(128)(4,1)}), s8[4194304]{0:T(1024)(128)(4,1)S(1)}, s32[]{:S(2)}) async-start(s8[12582912]{0:T(1024)(128)(4,1)} %bitcast.81), calls=%async_computation.4 | async-start | bytes 8388608
  247.0 9.1 %slice-start.1 = ((s8[12582912]{0:T(1024)(128)(4,1)}), s8[4194304]{0:T(1024)(128)(4,1)S(1)}, s32[]{:S(2)}) async-start(s8[12582912]{0:T(1024)(128)(4,1)} %bitcast.81), calls=%async_computation.5 | async-start | bytes 8388608
  251.5 4.6 %slice-start.2 = ((s8[12582912]{0:T(1024)(128)(4,1)}), s8[4194304]{0:T(1024)(128)(4,1)S(1)}, s32[]{:S(2)}) async-start(s8[12582912]{0:T(1024)(128)(4,1)} %bitcast.81), calls=%async_computation.6 | async-start | bytes 8388608
Sparse Core Ops, SparseCore 0:
  14.7 27.4 all-gather.5
  89.1 155.2 all-reduce.1
  374.1 51.7 reduce-scatter.3
